TPU v7x, 32 devices: a whole 2x2x4 slice. The times are simulated.
32 devices in a mesh: rows: 16 (over z, y, x), sub: 2 (over core).
Axes of the slice: x: 2, y: 2, z: 4, core: 2. Of those that a mesh axis runs over, the one named last changes fastest.
Arguments:
- matrix: float32 [4096, 384], P(('rows', 'sub')), as said below
- grad_out: float32 [4096, 384], P(('rows', 'sub')), as said below
- grad_factor: float32 [384, 384], replicated, may hold values from -6 to 6
Outputs:
- grad_matrix: float32 [4096, 384], P(('rows', 'sub'))
Inputs may be any that keep to these rules, and one draw needn't show every extreme that they name: `matrix`: entries at most of order 1 / sqrt(4096), with a scale that varies by row and by column. `grad_out`: entries of order 0.01.
All inputs are finite; a program needn't handle non-finite values.
Results may differ from a plain program's by a relative error of at most 0.0004.
Values sent between devices are 32-bit elements; how exact they have to be, the bound alone decides.
A program may use at most 64 MiB of HBM per device.

v0:
```python
import jax
import jax.numpy as jnp
from jax import lax
from jax.sharding import PartitionSpec as P

SECTIONS = 2


shift_frac = 0.02


def full_dot(left, right):
    return jnp.dot(left, right, precision=lax.Precision.HIGHEST, preferred_element_type=jnp.float32)


def inner_gram(left, right):
    return lax.dot_general(
        left,
        right,
        (((0,), (0,)), ((), ())),
        precision=lax.Precision.HIGHEST,
        preferred_element_type=jnp.float32,
    )


def cholesky_adjoint(lower_fac, lower_inv, lower_grad):
    product = full_dot(lower_fac.T, lower_grad)
    phi_part = jnp.tril(product) - 0.5 * jnp.diag(jnp.diag(product))
    sandwich = full_dot(full_dot(lower_inv.T, phi_part), lower_inv)
    return 0.5 * (sandwich + sandwich.T)


def factor_grads(uppers, grad_factor):
    count = len(uppers)
    result = []
    for section_index in range(count):
        middle = grad_factor
        for later in range(section_index + 1, count):
            middle = full_dot(uppers[later].T, middle)
        for earlier in range(section_index - 1, -1, -1):
            middle = full_dot(middle, uppers[earlier].T)
        result.append(middle)
    return result


def summed_gram(partial_value):
    half_rows = lax.psum_scatter(partial_value, "sub", scatter_dimension=0, tiled=True)
    half_rows = lax.psum(half_rows, "rows")
    return lax.all_gather(half_rows, "sub", axis=0, tiled=True)


def per_device(matrix, grad_out, grad_factor):
    width = matrix.shape[1]
    rate = shift_frac / width
    identity = jnp.eye(width, dtype=jnp.float32)
    current = matrix
    saved = []
    for section_index in range(SECTIONS):
        summed = summed_gram(inner_gram(current, current))
        shift_val = rate * jnp.trace(summed)
        lower_fac = jnp.linalg.cholesky(summed + shift_val * identity)
        lower_inv = lax.linalg.triangular_solve(lower_fac, identity, left_side=True, lower=True)
        following = full_dot(current, lower_inv.T)
        saved.append((current, following, lower_fac, lower_inv))
        current = following
    uppers = [item[2].T for item in saved]
    fac_grads = factor_grads(uppers, grad_factor)
    q_grad = grad_out
    for section_index in range(SECTIONS - 1, -1, -1):
        before, after, lower_fac, lower_inv = saved[section_index]
        crossed = lax.psum(inner_gram(after, q_grad), ("rows", "sub"))
        total_grad = fac_grads[section_index] - full_dot(crossed, lower_inv)
        gram_grad = cholesky_adjoint(lower_fac, lower_inv, jnp.tril(total_grad.T))
        gram_grad = gram_grad + rate * jnp.trace(gram_grad) * identity
        q_grad = full_dot(q_grad, lower_inv) + 2.0 * full_dot(before, gram_grad)
    return q_grad


def solution(mesh):
    placed = (P(("rows", "sub"), None), P(("rows", "sub"), None), P())
    return jax.shard_map(
        per_device, mesh=mesh, in_specs=placed, out_specs=P(("rows", "sub"), None), check_vma=False
    )
```

profile of v0, /device:TPU:29, one launch (start us, length us, event | category | flops | bytes accessed | tf_op | source)
XLA Modules:
  0.0 774.6 jit_solution(7228258176599560391)
XLA Ops:
  6.5 2.6 fusion.120
  9.2 10.1 %reduce-scatter.7.cloned.1.call-done = f32[192,384]{1,0:T(8,128)} async-done(((f32[384,384]{1,0:T(8,128)}), f32[192,384]{1,0:T(8,128)}) %reduce-scatter.7.cloned.1.call-update) | async-done | bytes 294928
  19.3 1.9 copy.59
  21.3 109.1 %all-reduce.6.cloned.1.call-done = f32[192,384]{0,1:T(8,128)} async-done(((f32[192,384]{0,1:T(8,128)}), f32[192,384]{0,1:T(8,128)}) %all-reduce.6.cloned.1.call-update) | async-done | bytes 294928 | tf_op jit(solution)/shard_map/psum | solution.py:48
  131.5 4.6 all_gather.6
  138.0 11.7 %cholesky.208 = f32[128,128]{1,0:T(8,128)S(1)} custom-call(f32[128,128]{1,0:T(8,128)S(1)} %cholesky.310), custom_call_target="Cholesky" | custom-call | tf_op jit(solution)/shard_map/jit(cholesky)/cholesky | solution.py:61
  149.7 9.8 %custom-call.24 = f32[1,128,128]{1,2,0:T(8,128)S(1)} custom-call(f32[1,128,128]{2,1,0:T(8,128)S(1)} %get-tuple-element.56), custom_call_target="InvertDiagBlocksLowerTriangular" | custom-call | tf_op jit(solution)/shard_map/jit(cholesky)/cholesky | solution.py:61
  160.2 11.7 %cholesky.227 = f32[128,128]{1,0:T(8,128)S(1)} custom-call(f32[128,128]{1,0:T(8,128)S(1)} %cholesky.314), custom_call_target="Cholesky" | custom-call | tf_op jit(solution)/shard_map/jit(cholesky)/cholesky | solution.py:61
  171.9 10.0 %custom-call.25 = f32[1,128,128]{1,2,0:T(8,128)S(1)} custom-call(f32[1,128,128]{2,1,0:T(8,128)S(1)} %get-tuple-element.53), custom_call_target="InvertDiagBlocksLowerTriangular" | custom-call | tf_op jit(solution)/shard_map/jit(cholesky)/cholesky | solution.py:61
  182.4 11.7 %cholesky.246 = f32[128,128]{1,0:T(8,128)S(1)} custom-call(f32[128,128]{1,0:T(8,128)S(1)} %convolution_subtract_fusion.9), custom_call_target="Cholesky" | custom-call | tf_op jit(solution)/shard_map/jit(cholesky)/cholesky | solution.py:61
  197.5 6.0 while.4
  198.1 1.3 bitcast_dynamic-update-slice_fusion.4
  200.1 1.3 bitcast_dynamic-update-slice_fusion.4
  202.1 1.3 bitcast_dynamic-update-slice_fusion.4
  203.4 29.5 %custom-call.26 = f32[3,128,128]{1,2,0:T(8,128)S(1)} custom-call(f32[3,128,128]{2,1,0:T(8,128)S(1)} %get-tuple-element.21), custom_call_target="InvertDiagBlocksLowerTriangular" | custom-call | tf_op jit(solution)/shard_map/triangular_solve/custom-call.2 | solution.py:62
  236.7 1.4 fusion.121
  238.2 8.6 %reduce-scatter.9.cloned.1.call-done = f32[192,384]{1,0:T(8,128)} async-done(((f32[384,384]{1,0:T(8,128)}), f32[192,384]{1,0:T(8,128)}) %reduce-scatter.9.cloned.1.call-update) | async-done | bytes 294928
  246.8 1.9 copy.61
  248.7 109.0 %all-reduce.8.cloned.1.call-done = f32[192,384]{0,1:T(8,128)} async-done(((f32[192,384]{0,1:T(8,128)}), f32[192,384]{0,1:T(8,128)}) %all-reduce.8.cloned.1.call-update) | async-done | bytes 294928 | tf_op jit(solution)/shard_map/psum | solution.py:48
  358.9 4.8 all_gather.7
  367.4 11.7 %cholesky.261 = f32[128,128]{1,0:T(8,128)S(1)} custom-call(f32[128,128]{1,0:T(8,128)S(1)} %cholesky.318), custom_call_target="Cholesky" | custom-call | tf_op jit(solution)/shard_map/jit(cholesky)/cholesky | solution.py:61
  379.2 9.8 %custom-call.27 = f32[1,128,128]{1,2,0:T(8,128)S(1)} custom-call(f32[1,128,128]{2,1,0:T(8,128)S(1)} %get-tuple-element.49), custom_call_target="InvertDiagBlocksLowerTriangular" | custom-call | tf_op jit(solution)/shard_map/jit(cholesky)/cholesky | solution.py:61
  389.6 11.7 %cholesky.280 = f32[128,128]{1,0:T(8,128)S(1)} custom-call(f32[128,128]{1,0:T(8,128)S(1)} %cholesky.322), custom_call_target="Cholesky" | custom-call | tf_op jit(solution)/shard_map/jit(cholesky)/cholesky | solution.py:61
  402.7 10.2 %custom-call.28 = f32[1,128,128]{1,2,0:T(8,128)S(1)} custom-call(f32[1,128,128]{2,1,0:T(8,128)S(1)} %get-tuple-element.46), custom_call_target="InvertDiagBlocksLowerTriangular" | custom-call | tf_op jit(solution)/shard_map/jit(cholesky)/cholesky | solution.py:61
  413.4 11.7 %cholesky.299 = f32[128,128]{1,0:T(8,128)S(1)} custom-call(f32[128,128]{1,0:T(8,128)S(1)} %convolution_subtract_fusion.8), custom_call_target="Cholesky" | custom-call | tf_op jit(solution)/shard_map/jit(cholesky)/cholesky | solution.py:61
  428.7 8.7 %while.5 = (s32[]{:T(128)}, f32[384,384]{1,0:T(8,128)}, s32[3,2]{0,1:T(2,128)S(1)}, f32[3,128,128]{2,1,0:T(8,128)S(1)}, s32[]{:T(128)}) while((s32[]{:T(128)}, f32[384,384]{1,0:T(8,128)}, s32[3,2]{0,1:T(2,128)S(1)}, f32[3,128,128]{2,1,0:T(8,128)S(1)}, s32[]{:T(128)}) %tuple.65), condition=%wide.while_cond.clone, body=%wide.while_body.clone.sunk | while | flops 2 | bytes 131181 | solution.py:62
  429.4 2.2 bitcast_dynamic-update-slice_fusion.5
  432.3 2.2 bitcast_dynamic-update-slice_fusion.5
  435.2 2.2 bitcast_dynamic-update-slice_fusion.5
  437.4 29.5 %custom-call.29 = f32[3,128,128]{1,2,0:T(8,128)S(1)} custom-call(f32[3,128,128]{2,1,0:T(8,128)S(1)} %get-tuple-element.22), custom_call_target="InvertDiagBlocksLowerTriangular" | custom-call | tf_op jit(solution)/shard_map/triangular_solve/custom-call.2 | solution.py:62
  467.6 1.3 convolution_subtract_fusion.3
  470.2 1.7 convolution_subtract_fusion.2
  474.1 1.5 fusion.122
  475.9 2.1 fusion.38
  478.0 124.6 %all-reduce.10.cloned.1.call-done = f32[384,384]{1,0:T(8,128)} async-done(((f32[384,384]{1,0:T(8,128)}), f32[384,384]{1,0:T(8,128)}) %all-reduce.10.cloned.1.call-update) | async-done | bytes 589840 | tf_op jit(solution)/shard_map/psum | solution.py:71
  602.6 2.5 fusion
  605.1 1.5 fusion.34
  607.7 3.4 gather_fusion
  611.1 3.3 fusion.21
  616.7 1.7 select_reduce_fusion.1
  619.0 1.8 convolution_multiply_fusion.1
  622.0 1.4 fusion.123
  624.8 127.6 %all-reduce.12.cloned.1.call-done = f32[384,384]{1,0:T(8,128)} async-done(((f32[384,384]{1,0:T(8,128)}), f32[384,384]{1,0:T(8,128)}) %all-reduce.12.cloned.1.call-update) | async-done | bytes 589840 | tf_op jit(solution)/shard_map/psum | solution.py:71
  752.4 2.4 fusion.1
  754.8 1.5 fusion.36
  756.5 3.7 gather_fusion.1
  760.2 2.1 fusion.14
  766.2 1.3 convolution_add_fusion
  (119 shorter events, 34.7 us)
Async XLA Ops:
  6.5 469.4 %copy-start = (f32[384,384]{1,0:T(8,128)S(1)}, f32[384,384]{1,0:T(8,128)}, u32[]{:S(2)}) copy-start(f32[384,384]{1,0:T(8,128)} %param.8) | copy-start | bytes 1769476
  6.5 12.7 %reduce-scatter.7.cloned.1.call-start = ((), (), s32[]{:S(2)}) async-start(), calls=%async_computation.6 | async-start | bytes 884736
  9.1 121.3 %all-reduce.6.cloned.1.call-start = ((), (), s32[]{:S(2)}) async-start(), calls=%async_computation.2 | async-start | bytes 786432 | tf_op jit(solution)/shard_map/psum | solution.py:48
  21.2 225.6 %reduce-scatter.9.cloned.1.call-start = ((), (), s32[]{:S(2)}) async-start(), calls=%async_computation.7 | async-start | bytes 884736
  21.3 213.0 %copy-start.1 = (f32[384,384]{0,1:T(8,128)}, f32[384,384]{0,1:T(8,128)S(1)}, u32[]{:S(2)}) copy-start(f32[384,384]{0,1:T(8,128)S(1)} %fusion.26) | copy-start | bytes 1769476
  235.1 0.9 copy-start.6
  238.1 119.6 %all-reduce.8.cloned.1.call-start = ((), (), s32[]{:S(2)}) async-start(), calls=%async_computation.3 | async-start | bytes 786432 | tf_op jit(solution)/shard_map/psum | solution.py:48
  248.7 353.9 %all-reduce.10.cloned.1.call-start = ((), (), s32[]{:S(2)}) async-start(), calls=%async_computation.4 | async-start | bytes 1179648 | tf_op jit(solution)/shard_map/psum | solution.py:71
  367.4 11.7 %copy-start.10 = (f32[384,384]{1,0:T(8,128)}, f32[384,384]{1,0:T(8,128)S(1)}, u32[]{:S(2)}) copy-start(f32[384,384]{1,0:T(8,128)S(1)} %fusion.6) | copy-start | bytes 1769476
  379.2 9.9 %copy-start.11 = (f32[384,384]{1,0:T(8,128)S(1)}, f32[384,384]{1,0:T(8,128)}, u32[]{:S(2)}) copy-start(f32[384,384]{1,0:T(8,128)} %copy-done.10) | copy-start | bytes 1769476
  427.8 39.1 %copy-start.2 = (f32[384,384]{0,1:T(8,128)S(1)}, f32[384,384]{0,1:T(8,128)}, u32[]{:S(2)}) copy-start(f32[384,384]{0,1:T(8,128)} %copy-done.1) | copy-start | bytes 1769476
  466.9 0.7 copy-start.14
  473.1 129.5 %copy-start.3 = (f32[128,384]{1,0:T(8,128)}, f32[128,384]{1,0:T(8,128)S(1)}, u32[]{:S(2)}) copy-start(f32[128,384]{1,0:T(8,128)S(1)} %fusion.76) | copy-start | bytes 589828
  473.1 1.0 copy-start.12
  475.7 276.7 %all-reduce.12.cloned.1.call-start = ((), (), s32[]{:S(2)}) async-start(), calls=%async_computation.5 | async-start | bytes 1179648 | tf_op jit(solution)/shard_map/psum | solution.py:71
  611.1 3.3 copy-start.4
  619.0 1.8 copy-start.5
  619.0 1.8 copy-start.13
  622.0 1.5 copy-start.8
  763.8 1.4 copy-start.7
  765.2 0.9 copy-start.9
Sparse Core Ops, SparseCore 0:
  9.6 9.6 reduce-scatter.6
  24.4 105.9 all-reduce.5
  238.2 8.4 reduce-scatter.8
  251.8 105.9 all-reduce.7
  475.8 126.7 all-reduce.9
  623.6 128.7 all-reduce.11
where the time goes:
time: 788 us; the launch traced here: 775 us
  waiting for transfers between devices  489 us (62%)
  other arithmetic  179 us (23%)
  matrix products  43.1 us (5%)
  local copies, waits for them, and re-layouts  33.2 us (4%)
  between operations  20.5 us (3%)
  blocking collectives  9.43 us (1%)
    psum x2, waiting for transfers between devices, per_device(): crossed = lax.psum(inner_gram(after, q_grad), ('rows', 'sub'))  252 us
    psum x2, waiting for transfers between devices, summed_gram(): half_rows = lax.psum(half_rows, 'rows')  218 us
    another operation x21, other arithmetic, per_device(): lower_fac = jnp.linalg.cholesky(summed + shift_val * identity)  114 us
    another operation x5, other arithmetic, per_device(): lax.linalg.triangular_solve(lower_fac, identity, left_side=True, lower=True)  59.9 us
    dot_general x16, matrix products, full_dot(): jnp.dot(left, right, precision=lax.Precision.HIGHEST, preferred_element_t...  25.6 us
    unnamed x8, waiting for transfers between devices  18.8 us
  transfers between devices with their start and end apart: 6, of which 6 were waited for; matrix products, arithmetic and copies ran while one was open for 0% of the time, Pallas kernels for 0%

commit v1 on v0

v1 whole, which is shorter than its diff:
```python
import functools

import jax
import jax.numpy as jnp
from jax import lax
from jax.experimental import pallas as pl
from jax.experimental.pallas import tpu as pltpu
from jax.sharding import PartitionSpec as P

LANES = 128
PANEL = 8
shift_frac = 0.02
VMEM_LIMIT = 56 * 1024 * 1024


def dot(left, right, dims=((1,), (0,))):
    return lax.dot_general(
        left, right, (dims, ((), ())), precision=lax.Precision.HIGHEST, preferred_element_type=jnp.float32
    )


def dot_tn(left, right):
    return dot(left, right, ((0,), (0,)))


def dot_nt(left, right):
    return dot(left, right, ((1,), (1,)))


def upper_pairs(count):
    return [(i, j) for i in range(count) for j in range(i, count)]


def block(index):
    return pl.ds(index * LANES, LANES)


def iotas(shape):
    return lax.broadcasted_iota(jnp.int32, shape, 0), lax.broadcasted_iota(jnp.int32, shape, 1)


def piece_rows(rows, devices):
    share = -(-rows // devices)
    return -(-share // 8) * 8


class Summer:
    def __init__(self, counts, rows):
        self.counts = counts
        self.devices = counts[0] * counts[1]
        self.piece = piece_rows(rows, self.devices)
        self.owners = -(-rows // self.piece)
        self.rows = self.owners * self.piece

    def scratch(self):
        return [
            pltpu.VMEM((self.rows, LANES), jnp.float32),
            pltpu.VMEM((self.devices - 1, self.piece, LANES), jnp.float32),
            pltpu.VMEM((self.rows, LANES), jnp.float32),
            pltpu.SemaphoreType.DMA((4,)),
        ]

    def bind(self, me, part, inbox, total, sems):
        self.me, self.part, self.inbox, self.total, self.sems = me, part, inbox, total, sems
        return self

    def peer(self, offset):
        return lax.rem(self.me + offset, self.devices)

    def place(self, device):
        return (device // self.counts[1], lax.rem(device, self.counts[1]))

    def rows_of(self, device):
        return pl.ds(pl.multiple_of(device * self.piece, 8), self.piece)

    def is_owner(self, device, action):
        if self.owners == self.devices:
            action()
        else:
            pl.when(device < self.owners)(action)

    def greet(self):
        barrier = pltpu.get_barrier_semaphore()

        def signal(offset, carry):
            pl.semaphore_signal(
                barrier, inc=1, device_id=self.place(self.peer(offset)), device_id_type=pl.DeviceIdType.MESH
            )
            return carry

        lax.fori_loop(1, self.devices, signal, 0)

    def greeted(self):
        pl.semaphore_wait(pltpu.get_barrier_semaphore(), self.devices - 1)

    def outgoing(self, offset):
        peer = self.peer(offset)
        return pltpu.make_async_remote_copy(
            src_ref=self.part.at[self.rows_of(peer)],
            dst_ref=self.inbox.at[offset - 1],
            send_sem=self.sems.at[0],
            recv_sem=self.sems.at[1],
            device_id=self.place(peer),
            device_id_type=pl.DeviceIdType.MESH,
        )

    def spread(self, offset):
        mine = self.total.at[self.rows_of(self.me)]
        return pltpu.make_async_remote_copy(
            src_ref=mine,
            dst_ref=mine,
            send_sem=self.sems.at[2],
            recv_sem=self.sems.at[3],
            device_id=self.place(self.peer(offset)),
            device_id_type=pl.DeviceIdType.MESH,
        )

    def each_peer(self, action):
        def step(offset, carry):
            action(offset)
            return carry

        lax.fori_loop(1, self.devices, step, 0)

    def start(self):
        self.each_peer(lambda offset: self.is_owner(self.peer(offset), lambda: self.outgoing(offset).start()))

    def reduce(self):
        def owned():
            pltpu.make_async_copy(self.inbox, self.inbox, self.sems.at[1]).wait()
            mine = self.rows_of(self.me)
            summed = self.part[mine, :]
            for slot in range(self.devices - 1):
                summed = summed + self.inbox[slot]
            self.total[mine, :] = summed
            self.each_peer(lambda offset: self.spread(offset).start())

        self.is_owner(self.me, owned)

    def wait_rows(self, rows):
        view = self.total.at[pl.ds(0, rows)]
        pltpu.make_async_copy(view, view, self.sems.at[3]).wait()

    def finish(self):
        if self.owners == self.devices:
            self.wait_rows(self.rows - self.piece)
        else:
            pl.when(self.me < self.owners)(lambda: self.wait_rows(self.rows - self.piece))
            pl.when(self.me >= self.owners)(lambda: self.wait_rows(self.rows))
        self.each_peer(lambda offset: self.is_owner(self.peer(offset), lambda: self.outgoing(offset).wait_send()))
        self.is_owner(self.me, lambda: self.each_peer(lambda offset: self.spread(offset).wait_send()))


def store_gram(part, source, pairs):
    for index, (i, j) in enumerate(pairs):
        part[block(index), :] = dot_tn(source[:, block(i)], source[:, block(j)])


def first_kernel(counts, pairs, matrix, gram, part, inbox, total, sems):
    me = lax.axis_index("rows") * counts[1] + lax.axis_index("sub")
    summer = Summer(counts, len(pairs) * LANES).bind(me, part, inbox, total, sems)
    summer.greet()
    store_gram(part, matrix, pairs)
    summer.greeted()
    summer.start()
    summer.reduce()
    summer.finish()
    gram[...] = total[pl.ds(0, len(pairs) * LANES), :]


def second_kernel(counts, pairs, current, q_grad, sums, part, inbox, total, sems):
    me = lax.axis_index("rows") * counts[1] + lax.axis_index("sub")
    width = current.shape[1] // LANES
    used = (len(pairs) + width * width) * LANES
    summer = Summer(counts, used).bind(me, part, inbox, total, sems)
    summer.greet()
    store_gram(part, current, pairs)
    for i in range(width):
        for j in range(width):
            slot = len(pairs) + i * width + j
            part[block(slot), :] = dot_tn(current[:, block(i)], q_grad[:, block(j)])
    if summer.rows > used:
        part[pl.ds(used, summer.rows - used), :] = jnp.zeros((summer.rows - used, LANES), jnp.float32)
    summer.greeted()
    summer.start()
    summer.reduce()
    summer.finish()
    sums[...] = total[pl.ds(0, used), :]


def factor_block(work):
    sub, lane = iotas((PANEL, LANES))

    def step(group, carry):
        top = group * PANEL
        rows = pl.ds(pl.multiple_of(top, PANEL), PANEL)
        left = work[rows, pl.ds(0, LANES)]
        right = work[rows, pl.ds(LANES, LANES)]
        rolled = pltpu.roll(left, lax.rem(LANES - top, LANES), 1)
        cols = [jnp.broadcast_to(rolled[:, k : k + 1], (PANEL, LANES)) for k in range(PANEL)]
        pivots = jnp.zeros((PANEL, LANES), jnp.float32)
        for k in range(PANEL):
            pivot = jnp.broadcast_to(cols[k][k : k + 1, :], (PANEL, LANES))
            pivots = jnp.where(sub == k, pivot, pivots)
            factor = jnp.where(sub > k, cols[k] / pivot, 0.0)
            for later in range(k + 1, PANEL):
                cols[later] = cols[later] - factor * jnp.broadcast_to(cols[later][k : k + 1, :], (PANEL, LANES))
            left = left - factor * jnp.broadcast_to(left[k : k + 1, :], (PANEL, LANES))
            right = right - factor * jnp.broadcast_to(right[k : k + 1, :], (PANEL, LANES))
        scale = 1.0 / jnp.sqrt(pivots)
        left = jnp.where(lane >= top + sub, left * scale, 0.0)
        right = right * scale
        both = jnp.concatenate([left, right], axis=1)
        below = jnp.where(lane >= top + PANEL, left, 0.0)
        work[...] = work[...] - dot_tn(below, both)
        work[rows, :] = both
        return carry

    lax.fori_loop(0, LANES // PANEL, step, 0)


def factor_all(width, gram, work, upper, inverse):
    pairs = upper_pairs(width)
    size = width * LANES
    rate = shift_frac / size
    row, lane = iotas((LANES, LANES))
    same = row == lane
    trace = jnp.float32(0.0)
    for index, (i, j) in enumerate(pairs):
        if i == j:
            trace = trace + jnp.sum(jnp.where(same, gram[block(index), :], 0.0))
    shift = rate * trace
    eye = jnp.where(same, 1.0, 0.0).astype(jnp.float32)
    zero = jnp.zeros((LANES, LANES), jnp.float32)
    for index, (i, j) in enumerate(pairs):
        piece = gram[block(index), :]
        upper[block(i), block(j)] = piece + shift * eye if i == j else piece
        if i != j:
            upper[block(j), block(i)] = zero
            inverse[block(i), block(j)] = zero
    for b in range(width):
        work[:, pl.ds(0, LANES)] = upper[block(b), block(b)]
        work[:, pl.ds(LANES, LANES)] = eye
        factor_block(work)
        upper[block(b), block(b)] = work[:, pl.ds(0, LANES)]
        inv = work[:, pl.ds(LANES, LANES)]
        inverse[block(b), block(b)] = inv
        for j in range(b + 1, width):
            upper[block(b), block(j)] = dot(inv, upper[block(b), block(j)])
        for i in range(b + 1, width):
            for j in range(i, width):
                upper[block(i), block(j)] = upper[block(i), block(j)] - dot_tn(
                    upper[block(b), block(i)], upper[block(b), block(j)]
                )
        for j in range(b):
            acc = zero
            for k in range(j, b):
                acc = acc + dot_tn(upper[block(k), block(b)], inverse[block(k), block(j)])
            inverse[block(b), block(j)] = -dot(inv, acc)


def section_kernel(width, gram, matrix, upper, inverse, following, work):
    factor_all(width, gram, work, upper, inverse)
    following[...] = dot_nt(matrix[...], inverse[...])


def gram_grad(upper, inverse, total_grad, rate):
    row, lane = iotas(total_grad.shape)
    lower_grad = jnp.where(row >= lane, total_grad.T, 0.0)
    product = dot(upper, lower_grad)
    phi = jnp.where(row > lane, product, jnp.where(row == lane, 0.5 * product, 0.0))
    sandwich = dot(dot_tn(inverse, phi), inverse)
    result = 0.5 * (sandwich + sandwich.T)
    trace = jnp.sum(jnp.where(row == lane, result, 0.0))
    return result + jnp.where(row == lane, rate * trace, 0.0)


def last_kernel(
    width, sums, upper1, inverse1, matrix, current, q_grad, grad_factor, out, work, upper2, inverse2, gram2, cross
):
    pairs = upper_pairs(width)
    rate = shift_frac / (width * LANES)
    factor_all(width, sums, work, upper2, inverse2)
    for index, (i, j) in enumerate(pairs):
        piece = sums[block(index), :]
        gram2[block(i), block(j)] = piece
        if i != j:
            gram2[block(j), block(i)] = piece.T
    for i in range(width):
        for j in range(width):
            cross[block(i), block(j)] = sums[block(len(pairs) + i * width + j), :]
    total2 = dot_nt(grad_factor[...], upper1[...]) - dot(dot(inverse2[...], cross[...]), inverse2[...])
    grad2 = gram_grad(upper2[...], inverse2[...], total2, rate)
    crossed1 = dot(cross[...], inverse2[...]) + 2.0 * dot(gram2[...], grad2)
    total1 = dot_tn(upper2[...], grad_factor[...]) - dot(crossed1, inverse1[...])
    grad1 = gram_grad(upper1[...], inverse1[...], total1, rate)
    middle = dot(q_grad[...], inverse2[...]) + 2.0 * dot(current[...], grad2)
    out[...] = dot(middle, inverse1[...]) + 2.0 * dot(matrix[...], grad1)


def per_device(counts, matrix, grad_out, grad_factor):
    rows, size = matrix.shape
    width = size // LANES
    pairs = upper_pairs(width)
    vmem = pl.BlockSpec(memory_space=pltpu.VMEM)
    square = jax.ShapeDtypeStruct((size, size), jnp.float32)
    tall = jax.ShapeDtypeStruct((rows, size), jnp.float32)
    square_scratch = pltpu.VMEM((size, size), jnp.float32)
    work = pltpu.VMEM((LANES, 2 * LANES), jnp.float32)

    def call(body, outs, args, scratch, **params):
        return pl.pallas_call(
            body,
            out_shape=outs,
            in_specs=[vmem] * len(args),
            out_specs=jax.tree.map(lambda _: vmem, outs),
            scratch_shapes=scratch,
            compiler_params=pltpu.CompilerParams(vmem_limit_bytes=VMEM_LIMIT, **params),
        )(*args)

    used = len(pairs) * LANES
    gram = call(
        functools.partial(first_kernel, counts, pairs),
        jax.ShapeDtypeStruct((used, LANES), jnp.float32),
        (matrix,),
        Summer(counts, used).scratch(),
        collective_id=0,
        has_side_effects=True,
    )
    upper1, inverse1, current = call(
        functools.partial(section_kernel, width), (square, square, tall), (gram, matrix), [work]
    )
    used = (len(pairs) + width * width) * LANES
    sums = call(
        functools.partial(second_kernel, counts, pairs),
        jax.ShapeDtypeStruct((used, LANES), jnp.float32),
        (current, grad_out),
        Summer(counts, used).scratch(),
        collective_id=1,
        has_side_effects=True,
    )
    return call(
        functools.partial(last_kernel, width),
        tall,
        (sums, upper1, inverse1, matrix, current, grad_out, grad_factor),
        [work] + [square_scratch] * 4,
    )


def solution(mesh):
    counts = (mesh.shape["rows"], mesh.shape["sub"])
    placed = (P(("rows", "sub"), None), P(("rows", "sub"), None), P())
    return jax.shard_map(
        functools.partial(per_device, counts),
        mesh=mesh,
        in_specs=placed,
        out_specs=P(("rows", "sub"), None),
        check_vma=False,
    )
```

time: 788 us -> 166 us (0.21); the launches traced: 775 us -> 165 us
  waiting for transfers between devices: 489 us -> 0 us
  other arithmetic: 179 us -> 0 us
  Pallas kernels: 0 us -> 165 us
  matrix products: 43.1 us -> 0 us
  local copies, waits for them, and re-layouts: 33.2 us -> 0 us
  between operations: 20.5 us -> 0.02 us
  blocking collectives: 9.43 us -> 0 us
    psum x4 -> x0, waiting for transfers between devices: 470 us -> none  [the longest x2 252 us: per_device(): crossed = lax.psum(inner_gram(after, q_grad), ('rows', 'sub'))]
    another operation x26 -> x0, other arithmetic: 174 us -> none  [the longest x21 114 us: per_device(): lower_fac = jnp.linalg.cholesky(summed + shift_val * identity)]
    pallas_call x0 -> x4, Pallas kernels: none -> 165 us  [call(): pl.pallas_call(body, out_shape=outs, in_specs=[vmem] * len(args), out_spe...]
    dot_general x18 -> x0, matrix products: 28.6 us -> none  [the longest x16 25.6 us: full_dot(): jnp.dot(left, right, precision=lax.Precision.HIGHEST, preferred_element_t...]
    unnamed x8 -> x0, waiting for transfers between devices: 18.8 us -> none
    another operation x27 -> x0, local copies, waits for them, and re-layouts: 14.7 us -> none  [the longest x21 14.6 us: per_device(): lax.linalg.triangular_solve(lower_fac, identity, left_side=True, lower=True)]
    another operation x18 -> x0, matrix products: 10.4 us -> none  [the longest x10 8.39 us: per_device(): lax.linalg.triangular_solve(lower_fac, identity, left_side=True, lower=True)]
    all_gather x2 -> x0, blocking collectives: 9.43 us -> none  [summed_gram(): return lax.all_gather(half_rows, 'sub', axis=0, tiled=True)]
  transfers between devices with their start and end apart: 6 -> 0, of which waited for: 6 -> 0; matrix products, arithmetic and copies ran while one was open for 0% -> 0% of each run, Pallas kernels for 0% -> 0%
where the time goes in v1:
time: 166 us; the launch traced here: 165 us
  Pallas kernels  165 us (99%)
    pallas_call x4, Pallas kernels, call(): pl.pallas_call(body, out_shape=outs, in_specs=[vmem] * len(args), out_spe...  165 us

profile of v1, /device:TPU:29, one launch (start us, length us, event | category | flops | bytes accessed | tf_op | source)
XLA Modules:
  0.0 165.3 jit_solution(14651230739118026505)
XLA Ops:
  0.0 27.1 %shard_map.37.gram = f32[768,128]{1,0:T(8,128)} custom-call(f32[128,384]{1,0:T(8,128)} %matrix.5), custom_call_target="tpu_custom_call" | custom-call | tf_op jit(solution)/shard_map/pallas_call | solution.py:312
  27.1 32.2 %shard_map.38 = (f32[384,384]{1,0:T(8,128)}, f32[384,384]{1,0:T(8,128)}, f32[128,384]{1,0:T(8,128)}) custom-call(f32[768,128]{1,0:T(8,128)} %shard_map.37.gram, f32[128,384]{1,0:T(8,128)} %matrix.5), custom_call_target="tpu_custom_call" | custom-call | tf_op jit(solution)/shard_map/pallas_call | solution.py:312
  59.2 55.9 %shard_map.39.sums = f32[1920,128]{1,0:T(8,128)} custom-call(f32[128,384]{1,0:T(8,128)} %get-tuple-element.8.current, f32[128,384]{1,0:T(8,128)} %q_grad.3), custom_call_target="tpu_custom_call" | custom-call | tf_op jit(solution)/shard_map/pallas_call | solution.py:312
  115.2 50.2 %shard_map.40 = f32[128,384]{1,0:T(8,128)} custom-call(f32[1920,128]{1,0:T(8,128)} %shard_map.39.sums, f32[384,384]{1,0:T(8,128)} %get-tuple-element.9.upper1, f32[384,384]{1,0:T(8,128)} %get-tuple-element.10.inverse1, f32[128,384]{1,0:T(8,128)} %matrix.5, f32[128,384]{1,0:T(8,128)} %get-tuple-element.8.current, f32[128,384]{1,0:T(8,128)} %q_grad.3, ...), custom_call_target="tpu_custom_call" | custom-call | tf_op jit(solution)/shard_map/pallas_call | solution.py:312

commit v2 on v1

--- a/solution.py
+++ b/solution.py
@@ -8,7 +8,7 @@
 from jax.sharding import PartitionSpec as P
 
 LANES = 128
-PANEL = 8
+PANEL = 16
 shift_frac = 0.02
 VMEM_LIMIT = 56 * 1024 * 1024
 
@@ -46,7 +46,7 @@
 
 class Summer:
     def __init__(self, counts, rows):
-        self.counts = counts
+        self.counts, self.used = counts, rows
         self.devices = counts[0] * counts[1]
         self.piece = piece_rows(rows, self.devices)
         self.owners = -(-rows // self.piece)
@@ -123,6 +123,9 @@
         lax.fori_loop(1, self.devices, step, 0)
 
     def start(self):
+        if self.rows > self.used:
+            spare = self.rows - self.used
+            self.part[pl.ds(self.used, spare), :] = jnp.zeros((spare, LANES), jnp.float32)
         self.each_peer(lambda offset: self.is_owner(self.peer(offset), lambda: self.outgoing(offset).start()))
 
     def reduce(self):
@@ -156,38 +159,6 @@
         part[block(index), :] = dot_tn(source[:, block(i)], source[:, block(j)])
 
 
-def first_kernel(counts, pairs, matrix, gram, part, inbox, total, sems):
-    me = lax.axis_index("rows") * counts[1] + lax.axis_index("sub")
-    summer = Summer(counts, len(pairs) * LANES).bind(me, part, inbox, total, sems)
-    summer.greet()
-    store_gram(part, matrix, pairs)
-    summer.greeted()
-    summer.start()
-    summer.reduce()
-    summer.finish()
-    gram[...] = total[pl.ds(0, len(pairs) * LANES), :]
-
-
-def second_kernel(counts, pairs, current, q_grad, sums, part, inbox, total, sems):
-    me = lax.axis_index("rows") * counts[1] + lax.axis_index("sub")
-    width = current.shape[1] // LANES
-    used = (len(pairs) + width * width) * LANES
-    summer = Summer(counts, used).bind(me, part, inbox, total, sems)
-    summer.greet()
-    store_gram(part, current, pairs)
-    for i in range(width):
-        for j in range(width):
-            slot = len(pairs) + i * width + j
-            part[block(slot), :] = dot_tn(current[:, block(i)], q_grad[:, block(j)])
-    if summer.rows > used:
-        part[pl.ds(used, summer.rows - used), :] = jnp.zeros((summer.rows - used, LANES), jnp.float32)
-    summer.greeted()
-    summer.start()
-    summer.reduce()
-    summer.finish()
-    sums[...] = total[pl.ds(0, used), :]
-
-
 def factor_block(work):
     sub, lane = iotas((PANEL, LANES))
 
@@ -198,16 +169,15 @@
         right = work[rows, pl.ds(LANES, LANES)]
         rolled = pltpu.roll(left, lax.rem(LANES - top, LANES), 1)
         cols = [jnp.broadcast_to(rolled[:, k : k + 1], (PANEL, LANES)) for k in range(PANEL)]
-        pivots = jnp.zeros((PANEL, LANES), jnp.float32)
+        scale = jnp.zeros((PANEL, LANES), jnp.float32)
         for k in range(PANEL):
-            pivot = jnp.broadcast_to(cols[k][k : k + 1, :], (PANEL, LANES))
-            pivots = jnp.where(sub == k, pivot, pivots)
-            factor = jnp.where(sub > k, cols[k] / pivot, 0.0)
+            root = lax.rsqrt(cols[k][k : k + 1, :])
+            scale = jnp.where(sub == k, root, scale)
+            factor = jnp.where(sub > k, cols[k] * root, 0.0)
             for later in range(k + 1, PANEL):
-                cols[later] = cols[later] - factor * jnp.broadcast_to(cols[later][k : k + 1, :], (PANEL, LANES))
-            left = left - factor * jnp.broadcast_to(left[k : k + 1, :], (PANEL, LANES))
-            right = right - factor * jnp.broadcast_to(right[k : k + 1, :], (PANEL, LANES))
-        scale = 1.0 / jnp.sqrt(pivots)
+                cols[later] = cols[later] - factor * (cols[later][k : k + 1, :] * root)
+            left = left - factor * (left[k : k + 1, :] * root)
+            right = right - factor * (right[k : k + 1, :] * root)
         left = jnp.where(lane >= top + sub, left * scale, 0.0)
         right = right * scale
         both = jnp.concatenate([left, right], axis=1)
@@ -219,7 +189,7 @@
     lax.fori_loop(0, LANES // PANEL, step, 0)
 
 
-def factor_all(width, gram, work, upper, inverse):
+def factor_all(width, gram, work, upper, inverse, after_block=lambda b: None):
     pairs = upper_pairs(width)
     size = width * LANES
     rate = shift_frac / size
@@ -257,11 +227,7 @@
             for k in range(j, b):
                 acc = acc + dot_tn(upper[block(k), block(b)], inverse[block(k), block(j)])
             inverse[block(b), block(j)] = -dot(inv, acc)
-
-
-def section_kernel(width, gram, matrix, upper, inverse, following, work):
-    factor_all(width, gram, work, upper, inverse)
-    following[...] = dot_nt(matrix[...], inverse[...])
+        after_block(b)
 
 
 def gram_grad(upper, inverse, total_grad, rate):
@@ -275,76 +241,83 @@
     return result + jnp.where(row == lane, rate * trace, 0.0)
 
 
-def last_kernel(
-    width, sums, upper1, inverse1, matrix, current, q_grad, grad_factor, out, work, upper2, inverse2, gram2, cross
-):
+def whole_kernel(counts, width, matrix, q_grad, grad_factor, out, *scratch):
+    gram_sum, later_sum, cross_sum = scratch[0:4], scratch[4:8], scratch[8:12]
+    work, upper1, inverse1, upper2, inverse2, current, square = scratch[12:]
+    me = lax.axis_index("rows") * counts[1] + lax.axis_index("sub")
     pairs = upper_pairs(width)
+    used = len(pairs) * LANES
     rate = shift_frac / (width * LANES)
-    factor_all(width, sums, work, upper2, inverse2)
-    for index, (i, j) in enumerate(pairs):
-        piece = sums[block(index), :]
-        gram2[block(i), block(j)] = piece
-        if i != j:
-            gram2[block(j), block(i)] = piece.T
+    first = Summer(counts, used).bind(me, *gram_sum)
+    second = Summer(counts, used).bind(me, *later_sum)
+    cross = Summer(counts, width * width * LANES).bind(me, *cross_sum)
+
+    first.greet()
+    store_gram(first.part, matrix, pairs)
+    first.greeted()
+    first.start()
+    first.reduce()
+    first.finish()
+    factor_all(width, first.total, work, upper1, inverse1)
+    current[...] = dot_nt(matrix[...], inverse1[...])
+
+    store_gram(second.part, current, pairs)
+    second.start()
     for i in range(width):
         for j in range(width):
-            cross[block(i), block(j)] = sums[block(len(pairs) + i * width + j), :]
-    total2 = dot_nt(grad_factor[...], upper1[...]) - dot(dot(inverse2[...], cross[...]), inverse2[...])
+            cross.part[block(i * width + j), :] = dot_tn(current[:, block(i)], q_grad[:, block(j)])
+    second.reduce()
+    second.finish()
+    cross.start()
+
+    def after_block(b):
+        if b == width - 2:
+            cross.reduce()
+
+    factor_all(width, second.total, work, upper2, inverse2, after_block)
+    factor2 = dot_nt(grad_factor[...], upper1[...])
+    factor1 = dot_tn(upper2[...], grad_factor[...])
+    moved = dot(q_grad[...], inverse2[...])
+    cross.finish()
+    for i in range(width):
+        for j in range(width):
+            square[block(i), block(j)] = cross.total[block(i * width + j), :]
+    turned = dot(square[...], inverse2[...])
+    total2 = factor2 - dot(inverse2[...], turned)
     grad2 = gram_grad(upper2[...], inverse2[...], total2, rate)
-    crossed1 = dot(cross[...], inverse2[...]) + 2.0 * dot(gram2[...], grad2)
-    total1 = dot_tn(upper2[...], grad_factor[...]) - dot(crossed1, inverse1[...])
+    for index, (i, j) in enumerate(pairs):
+        piece = second.total[block(index), :]
+        square[block(i), block(j)] = piece
+        if i != j:
+            square[block(j), block(i)] = piece.T
+    crossed1 = turned + 2.0 * dot(square[...], grad2)
+    total1 = factor1 - dot(crossed1, inverse1[...])
     grad1 = gram_grad(upper1[...], inverse1[...], total1, rate)
-    middle = dot(q_grad[...], inverse2[...]) + 2.0 * dot(current[...], grad2)
+    middle = moved + 2.0 * dot(current[...], grad2)
     out[...] = dot(middle, inverse1[...]) + 2.0 * dot(matrix[...], grad1)
 
 
 def per_device(counts, matrix, grad_out, grad_factor):
     rows, size = matrix.shape
     width = size // LANES
-    pairs = upper_pairs(width)
+    used = len(upper_pairs(width)) * LANES
     vmem = pl.BlockSpec(memory_space=pltpu.VMEM)
-    square = jax.ShapeDtypeStruct((size, size), jnp.float32)
-    tall = jax.ShapeDtypeStruct((rows, size), jnp.float32)
-    square_scratch = pltpu.VMEM((size, size), jnp.float32)
+    square = pltpu.VMEM((size, size), jnp.float32)
+    tall = pltpu.VMEM((rows, size), jnp.float32)
     work = pltpu.VMEM((LANES, 2 * LANES), jnp.float32)
-
-    def call(body, outs, args, scratch, **params):
-        return pl.pallas_call(
-            body,
-            out_shape=outs,
-            in_specs=[vmem] * len(args),
-            out_specs=jax.tree.map(lambda _: vmem, outs),
-            scratch_shapes=scratch,
-            compiler_params=pltpu.CompilerParams(vmem_limit_bytes=VMEM_LIMIT, **params),
-        )(*args)
-
-    used = len(pairs) * LANES
-    gram = call(
-        functools.partial(first_kernel, counts, pairs),
-        jax.ShapeDtypeStruct((used, LANES), jnp.float32),
-        (matrix,),
-        Summer(counts, used).scratch(),
-        collective_id=0,
-        has_side_effects=True,
+    sums = (
+        Summer(counts, used).scratch() + Summer(counts, used).scratch() + Summer(counts, width * size).scratch()
     )
-    upper1, inverse1, current = call(
-        functools.partial(section_kernel, width), (square, square, tall), (gram, matrix), [work]
-    )
-    used = (len(pairs) + width * width) * LANES
-    sums = call(
-        functools.partial(second_kernel, counts, pairs),
-        jax.ShapeDtypeStruct((used, LANES), jnp.float32),
-        (current, grad_out),
-        Summer(counts, used).scratch(),
-        collective_id=1,
-        has_side_effects=True,
-    )
-    return call(
-        functools.partial(last_kernel, width),
-        tall,
-        (sums, upper1, inverse1, matrix, current, grad_out, grad_factor),
-        [work] + [square_scratch] * 4,
-    )
+    return pl.pallas_call(
+        functools.partial(whole_kernel, counts, width),
+        out_shape=jax.ShapeDtypeStruct((rows, size), jnp.float32),
+        in_specs=[vmem] * 3,
+        out_specs=vmem,
+        scratch_shapes=sums + [work] + [square] * 4 + [tall, square],
+        compiler_params=pltpu.CompilerParams(
+            vmem_limit_bytes=VMEM_LIMIT, collective_id=0, has_side_effects=True
+        ),
+    )(matrix, grad_out, grad_factor)
 
 
 def solution(mesh):

time: 166 us -> 116 us (0.70)
  Pallas kernels: 165 us -> 114 us
    pallas_call x4 -> x1, Pallas kernels: 165 us -> 114 us  [per_device(): pl.pallas_call(functools.partial(whole_kernel, counts, width), out_shape=...]
where the time goes in v2:
time: 116 us
  Pallas kernels  114 us (98%)
  local copies, waits for them, and re-layouts  1.62 us (1%)
    pallas_call x1, Pallas kernels, per_device(): pl.pallas_call(functools.partial(whole_kernel, counts, width), out_shape=...  114 us

profile of v2, /device:TPU:29, one launch (start us, length us, event | category | flops | bytes accessed | tf_op | source)
XLA Modules:
  0.0 115.7 jit_solution(10459971413820999493)
XLA Ops:
  0.0 114.1 %shard_map.37 = f32[128,384]{1,0:T(8,128)} custom-call(f32[128,384]{1,0:T(8,128)} %matrix.1, f32[128,384]{1,0:T(8,128)} %q_grad.1, f32[384,384]{1,0:T(8,128)} %grad_factor.1), custom_call_target="tpu_custom_call" | custom-call | tf_op jit(solution)/shard_map/pallas_call | solution.py:311
  114.1 1.6 %copy.5 = f32[128,384]{1,0:T(8,128)} copy(f32[128,384]{1,0:T(8,128)} %shard_map.37) | data formatting | bytes 393216

commit v3 on v2

--- a/solution.py
+++ b/solution.py
@@ -17,6 +17,28 @@
     return lax.dot_general(
         left, right, (dims, ((), ())), precision=lax.Precision.HIGHEST, preferred_element_type=jnp.float32
     )
+
+
+def halves(value):
+    high = value.astype(jnp.bfloat16)
+    return high, (value - high.astype(jnp.float32)).astype(jnp.bfloat16)
+
+
+def dot3(left, right, dims=((1,), (0,))):
+    (left_high, left_low), (right_high, right_low) = halves(left), halves(right)
+
+    def product(a, b):
+        return lax.dot_general(a, b, (dims, ((), ())), preferred_element_type=jnp.float32)
+
+    return product(left_high, right_high) + (product(left_high, right_low) + product(left_low, right_high))
+
+
+def dot3_tn(left, right):
+    return dot3(left, right, ((0,), (0,)))
+
+
+def dot3_nt(left, right):
+    return dot3(left, right, ((1,), (1,)))
 
 
 def dot_tn(left, right):
@@ -165,9 +187,13 @@
     def step(group, carry):
         top = group * PANEL
         rows = pl.ds(pl.multiple_of(top, PANEL), PANEL)
-        left = work[rows, pl.ds(0, LANES)]
-        right = work[rows, pl.ds(LANES, LANES)]
-        rolled = pltpu.roll(left, lax.rem(LANES - top, LANES), 1)
+        waiting, source = carry
+        turn = lax.rem(LANES - top, LANES)
+        others = work[...] - dot_tn(waiting, source)
+        ahead = pltpu.roll(waiting, turn, 1)[:, 0:PANEL]
+        panel = work[rows, :] - dot_tn(ahead, source)
+        left, right = panel[:, 0:LANES], panel[:, LANES:]
+        rolled = pltpu.roll(left, turn, 1)
         cols = [jnp.broadcast_to(rolled[:, k : k + 1], (PANEL, LANES)) for k in range(PANEL)]
         scale = jnp.zeros((PANEL, LANES), jnp.float32)
         for k in range(PANEL):
@@ -182,11 +208,12 @@
         right = right * scale
         both = jnp.concatenate([left, right], axis=1)
         below = jnp.where(lane >= top + PANEL, left, 0.0)
-        work[...] = work[...] - dot_tn(below, both)
+        work[...] = others
         work[rows, :] = both
-        return carry
-
-    lax.fori_loop(0, LANES // PANEL, step, 0)
+        return below, both
+
+    none = jnp.zeros((PANEL, LANES), jnp.float32), jnp.zeros((PANEL, 2 * LANES), jnp.float32)
+    lax.fori_loop(0, LANES // PANEL, step, none)
 
 
 def factor_all(width, gram, work, upper, inverse, after_block=lambda b: None):
@@ -233,9 +260,9 @@
 def gram_grad(upper, inverse, total_grad, rate):
     row, lane = iotas(total_grad.shape)
     lower_grad = jnp.where(row >= lane, total_grad.T, 0.0)
-    product = dot(upper, lower_grad)
+    product = dot3(upper, lower_grad)
     phi = jnp.where(row > lane, product, jnp.where(row == lane, 0.5 * product, 0.0))
-    sandwich = dot(dot_tn(inverse, phi), inverse)
+    sandwich = dot3(dot3_tn(inverse, phi), inverse)
     result = 0.5 * (sandwich + sandwich.T)
     trace = jnp.sum(jnp.where(row == lane, result, 0.0))
     return result + jnp.where(row == lane, rate * trace, 0.0)
@@ -243,7 +270,7 @@
 
 def whole_kernel(counts, width, matrix, q_grad, grad_factor, out, *scratch):
     gram_sum, later_sum, cross_sum = scratch[0:4], scratch[4:8], scratch[8:12]
-    work, upper1, inverse1, upper2, inverse2, current, square = scratch[12:]
+    work, upper1, inverse1, upper2, inverse2, current, square, held = scratch[12:]
     me = lax.axis_index("rows") * counts[1] + lax.axis_index("sub")
     pairs = upper_pairs(width)
     used = len(pairs) * LANES
@@ -266,6 +293,7 @@
     for i in range(width):
         for j in range(width):
             cross.part[block(i * width + j), :] = dot_tn(current[:, block(i)], q_grad[:, block(j)])
+    held[...] = dot3_nt(grad_factor[...], upper1[...])
     second.reduce()
     second.finish()
     cross.start()
@@ -275,26 +303,25 @@
             cross.reduce()
 
     factor_all(width, second.total, work, upper2, inverse2, after_block)
-    factor2 = dot_nt(grad_factor[...], upper1[...])
-    factor1 = dot_tn(upper2[...], grad_factor[...])
-    moved = dot(q_grad[...], inverse2[...])
+    factor1 = dot3_tn(upper2[...], grad_factor[...])
+    moved = dot3(q_grad[...], inverse2[...])
     cross.finish()
     for i in range(width):
         for j in range(width):
             square[block(i), block(j)] = cross.total[block(i * width + j), :]
-    turned = dot(square[...], inverse2[...])
-    total2 = factor2 - dot(inverse2[...], turned)
+    turned = dot3(square[...], inverse2[...])
+    total2 = held[...] - dot3(inverse2[...], turned)
     grad2 = gram_grad(upper2[...], inverse2[...], total2, rate)
     for index, (i, j) in enumerate(pairs):
         piece = second.total[block(index), :]
         square[block(i), block(j)] = piece
         if i != j:
             square[block(j), block(i)] = piece.T
-    crossed1 = turned + 2.0 * dot(square[...], grad2)
-    total1 = factor1 - dot(crossed1, inverse1[...])
+    crossed1 = turned + 2.0 * dot3(square[...], grad2)
+    total1 = factor1 - dot3(crossed1, inverse1[...])
     grad1 = gram_grad(upper1[...], inverse1[...], total1, rate)
-    middle = moved + 2.0 * dot(current[...], grad2)
-    out[...] = dot(middle, inverse1[...]) + 2.0 * dot(matrix[...], grad1)
+    middle = moved + 2.0 * dot3(current[...], grad2)
+    out[...] = dot3(middle, inverse1[...]) + 2.0 * dot3(matrix[...], grad1)
 
 
 def per_device(counts, matrix, grad_out, grad_factor):
@@ -313,7 +340,7 @@
         out_shape=jax.ShapeDtypeStruct((rows, size), jnp.float32),
         in_specs=[vmem] * 3,
         out_specs=vmem,
-        scratch_shapes=sums + [work] + [square] * 4 + [tall, square],
+        scratch_shapes=sums + [work] + [square] * 4 + [tall, square, square],
         compiler_params=pltpu.CompilerParams(
             vmem_limit_bytes=VMEM_LIMIT, collective_id=0, has_side_effects=True
         ),

time: 116 us -> 109 us (0.940)
  Pallas kernels: 114 us -> 108 us
    pallas_call x1, Pallas kernels: 114 us -> 108 us  [per_device(): pl.pallas_call(functools.partial(whole_kernel, counts, width), out_shape=...]
where the time goes in v3:
time: 109 us
  Pallas kernels  108 us (99%)
  local copies, waits for them, and re-layouts  1.62 us (1%)
    pallas_call x1, Pallas kernels, per_device(): pl.pallas_call(functools.partial(whole_kernel, counts, width), out_shape=...  108 us

profile of v3, /device:TPU:29, one launch (start us, length us, event | category | flops | bytes accessed | tf_op | source)
XLA Modules:
  0.0 109.3 jit_solution(17113473755647507737)
XLA Ops:
  0.0 107.7 %shard_map.37 = f32[128,384]{1,0:T(8,128)} custom-call(f32[128,384]{1,0:T(8,128)} %matrix.1, f32[128,384]{1,0:T(8,128)} %q_grad.1, f32[384,384]{1,0:T(8,128)} %grad_factor.1), custom_call_target="tpu_custom_call" | custom-call | tf_op jit(solution)/shard_map/pallas_call | solution.py:338
  107.7 1.6 %copy.5 = f32[128,384]{1,0:T(8,128)} copy(f32[128,384]{1,0:T(8,128)} %shard_map.37) | data formatting | bytes 393216
